TPU v7x, 64 devices: a 2x2x8 block of a 4x4x8 slice. The times are simulated.
64 devices in a mesh: rep: 4 (over x, y), dp: 16 (over z, core).
Axes of the slice: x: 2, y: 2, z: 8, core: 2. Of those that a mesh axis runs over, the one named last changes fastest.
The devices are a block of a 4x4x8 slice.
Arguments:
- g_w_gate: bfloat16 [64, 2, 896, 3584], P(('rep', 'dp')), parts along dimension 0
- g_w_up: bfloat16 [64, 2, 896, 3584], P(('rep', 'dp')), parts along dimension 0
- g_w_down: bfloat16 [64, 2, 3584, 896], P(('rep', 'dp')), parts along dimension 0
- w_gate: bfloat16 [2, 896, 3584], replicated
- w_up: bfloat16 [2, 896, 3584], replicated
- w_down: bfloat16 [2, 3584, 896], replicated
- m_w_gate: float32 [2, 896, 3584], P(None, 'dp')
- m_w_up: float32 [2, 896, 3584], P(None, 'dp')
- m_w_down: float32 [2, 3584, 896], P(None, 'dp')
- v_w_gate: float32 [2, 896, 3584], P(None, 'dp')
- v_w_up: float32 [2, 896, 3584], P(None, 'dp')
- v_w_down: float32 [2, 3584, 896], P(None, 'dp')
Outputs:
- output 1: bfloat16 [8, 896, 3584], P('rep'), parts along dimension 0
- output 2: bfloat16 [8, 896, 3584], P('rep'), parts along dimension 0
- output 3: bfloat16 [8, 3584, 896], P('rep'), parts along dimension 0
- output 4: float32 [8, 896, 3584], P('rep', 'dp'), parts along dimension 0
- output 5: float32 [8, 896, 3584], P('rep', 'dp'), parts along dimension 0
- output 6: float32 [8, 3584, 896], P('rep', 'dp'), parts along dimension 0
- output 7: float32 [8, 896, 3584], P('rep', 'dp'), parts along dimension 0
- output 8: float32 [8, 896, 3584], P('rep', 'dp'), parts along dimension 0
- output 9: float32 [8, 3584, 896], P('rep', 'dp'), parts along dimension 0
There are 4 independent parts. A program takes and returns all parts, laid end to end along the dimension named above; an argument that names none is the same for every part.
All inputs are finite; a program needn't handle non-finite values.
Results may differ from a plain program's by a relative error of at most 0.022.
Values are sent between devices in bfloat16 or wider.
A program may use at most 768 MiB of HBM per device.

v0:
```python
import jax
import jax.numpy as jnp
from jax import lax
from jax.sharding import PartitionSpec as P


def adamw(w, m, v, g):
    m = 0.9 * m + 0.1 * g
    v = 0.95 * v + 0.05 * g * g
    step = m * lax.rsqrt(v + 1e-8) + 0.1 * w
    return (w - 0.02 * step).astype(jnp.bfloat16), m, v


def clipped(gradients, sum_of_squares, count):
    factor = jnp.minimum(1.0, 0.5 * lax.rsqrt(sum_of_squares / count + 1e-30))
    return [g * factor for g in gradients]


def solution(mesh):
    def step(*arrays):
        terms, weights, m, v = (arrays[i : i + 3] for i in (0, 3, 6, 9))
        gradients = [lax.psum_scatter(t[0], "dp", scatter_dimension=1, tiled=True).astype(jnp.float32) for t in terms]
        squares = lax.psum(sum(jnp.sum(g * g) for g in gradients), "dp")
        gradients = clipped(gradients, squares, lax.psum(1, "dp") * sum(g.size for g in gradients))
        me = lax.axis_index("dp")
        own = [lax.dynamic_slice_in_dim(w, me * one.shape[1], one.shape[1], 1).astype(jnp.float32) for w, one in zip(weights, m, strict=True)]
        new = [adamw(w, m, v, g) for w, m, v, g in zip(own, m, v, gradients, strict=True)]
        whole = [lax.all_gather(one[0], "dp", axis=1, tiled=True) for one in new]
        return (*whole, *(one[1] for one in new), *(one[2] for one in new))

    all_of, cut = P(None, None, None), P(None, "dp", None)
    return jax.shard_map(
        step,
        mesh=mesh,
        in_specs=(P(("rep", "dp"), None, None, None),) * 3 + (all_of,) * 3 + (cut,) * 6,
        out_specs=(P("rep", None, None),) * 3 + (P("rep", "dp", None),) * 6,
        check_vma=False,
    )
```

profile of v0, /device:TPU:21, one launch (start us, length us, event | category | flops | bytes accessed | tf_op | source)
XLA Modules:
  0.0 598.7 jit_solution(11980393026291308799)
XLA Ops:
  7.3 55.8 %copy.21 = bf16[2,896,3584]{2,0,1:T(2,128)(2,1)S(1)} copy(bf16[2,896,3584]{2,1,0:T(8,128)(2,1)} %bitcast.15) | data formatting | bytes 25690112
  63.1 5.5 copy.25
  68.7 55.8 %copy.23 = bf16[2,896,3584]{2,0,1:T(2,128)(2,1)S(1)} copy(bf16[2,896,3584]{2,1,0:T(8,128)(2,1)} %bitcast.16) | data formatting | bytes 25690112
  124.5 5.5 copy.26
  130.1 0.7 reduce-scatter.8.cloned.1.call-update
  130.9 19.3 %reduce-scatter.10.cloned.1.call-done = bf16[56,7168]{1,0:T(8,128)(2,1)} async-done(((bf16[896,7168]{1,0:T(8,128)(2,1)}), bf16[56,7168]{1,0:T(8,128)(2,1)}) %reduce-scatter.10.cloned.1.call-update) | async-done | bytes 802832
  150.1 2.6 reshape.19
  152.8 77.3 %reduce-scatter.12.cloned.1.call-done = bf16[56,7168]{1,0:T(8,128)(2,1)} async-done(((bf16[896,7168]{1,0:T(8,128)(2,1)}), bf16[56,7168]{1,0:T(8,128)(2,1)}) %reduce-scatter.12.cloned.1.call-update) | async-done | bytes 802832
  230.1 2.6 reshape.21
  232.7 1.0 fusion.9
  235.0 74.5 %reduce-scatter.8.cloned.1.call-done = bf16[2,224,896]{2,1,0:T(8,128)(2,1)} async-done(((bf16[2,3584,896]{2,1,0:T(8,128)(2,1)}), bf16[2,224,896]{2,1,0:T(8,128)(2,1)}) %reduce-scatter.8.cloned.1.call-update) | async-done | bytes 802832 | tf_op jit(solution)/shard_map/reduce_scatter | solution.py:22
  309.5 2.2 fusion.11
  312.3 24.7 %psum.7 = f32[]{:T(128)} all-reduce(f32[]{:T(128)S(6)} %add.65), channel_id=1, replica_groups=mesh['rep'=4,'dp'=16] {'dp'}, use_global_device_ids=true, to_apply=%region_6.0 | all-reduce | flops 1 | bytes 8 | tf_op jit(solution)/shard_map/psum | solution.py:23
  337.8 4.3 fusion.17
  342.4 4.7 fusion.8
  347.2 4.1 fusion.14
  351.3 66.0 %all-gather.8.cloned.1.call-done = bf16[2,3584,896]{2,1,0:T(8,128)(2,1)} async-done(((bf16[2,224,896]{2,1,0:T(8,128)(2,1)}), bf16[2,3584,896]{2,1,0:T(8,128)(2,1)}) %all-gather.8.cloned.1.call-update) | async-done | bytes 12845072 | tf_op jit(solution)/shard_map/all_gather | solution.py:28
  417.3 74.1 %all-gather.4.cloned.1.call-done = bf16[2,896,3584]{2,1,0:T(8,128)(2,1)} async-done(((bf16[2,56,3584]{2,1,0:T(8,128)(2,1)}), bf16[2,896,3584]{2,1,0:T(8,128)(2,1)}) %all-gather.4.cloned.1.call-update) | async-done | bytes 12845072 | tf_op jit(solution)/shard_map/all_gather | solution.py:28
  491.4 74.1 %all-gather.6.cloned.1.call-done = bf16[2,896,3584]{2,1,0:T(8,128)(2,1)} async-done(((bf16[2,56,3584]{2,1,0:T(8,128)(2,1)}), bf16[2,896,3584]{2,1,0:T(8,128)(2,1)}) %all-gather.6.cloned.1.call-update) | async-done | bytes 12845072 | tf_op jit(solution)/shard_map/all_gather | solution.py:28
  565.6 12.5 %copy.40 = bf16[2,896,3584]{2,1,0:T(8,128)(2,1)} copy(bf16[2,896,3584]{2,1,0:T(8,128)(2,1)} %all-gather.4.cloned.1.call-done) | data formatting | bytes 25690112
  578.1 6.5 %copy.41 = bf16[2,896,3584]{2,1,0:T(8,128)(2,1)} copy(bf16[2,896,3584]{2,1,0:T(8,128)(2,1)S(1)} %copy-done) | data formatting | bytes 25690112
  584.6 1.2 slice-done.1
  585.7 1.3 slice-done.2
  587.0 4.9 copy.42
  (24 shorter events, 0.9 us)
Async XLA Ops:
  7.2 143.0 %reduce-scatter.10.cloned.1.call-start = ((), (), s32[]{:S(2)}) async-start(), calls=%async_computation.7 | async-start | bytes 13647872
  68.6 161.5 %reduce-scatter.12.cloned.1.call-start = ((), (), s32[]{:S(2)}) async-start(), calls=%async_computation.8 | async-start | bytes 13647872
  130.0 179.5 %reduce-scatter.8.cloned.1.call-start = ((), (), s32[]{:S(2)}) async-start(), calls=%async_computation.3 | async-start | bytes 13647872 | tf_op jit(solution)/shard_map/reduce_scatter | solution.py:22
  130.8 286.5 %all-gather.8.cloned.1.call-start = ((), (), s32[]{:S(2)}) async-start(), calls=%async_computation.6 | async-start | bytes 13647872 | tf_op jit(solution)/shard_map/all_gather | solution.py:28
  232.7 105.1 %copy-start.1 = (f32[2,224,896]{2,1,0:T(8,128)S(1)}, f32[2,224,896]{2,1,0:T(8,128)}, u32[]{:S(2)}) copy-start(f32[2,224,896]{2,1,0:T(8,128)} %param.23) | copy-start | bytes 4816900
  342.1 149.3 %all-gather.4.cloned.1.call-start = ((), (), s32[]{:S(2)}) async-start(), calls=%async_computation.4 | async-start | bytes 13647872 | tf_op jit(solution)/shard_map/all_gather | solution.py:28
  342.4 4.8 copy-start.2
  347.1 218.4 %all-gather.6.cloned.1.call-start = ((), (), s32[]{:S(2)}) async-start(), calls=%async_computation.5 | async-start | bytes 13647872 | tf_op jit(solution)/shard_map/all_gather | solution.py:28
  565.6 12.5 %copy-start = (bf16[2,896,3584]{2,1,0:T(8,128)(2,1)S(1)}, bf16[2,896,3584]{2,1,0:T(8,128)(2,1)}, u32[]{:S(2)}) copy-start(bf16[2,896,3584]{2,1,0:T(8,128)(2,1)} %all-gather.6.cloned.1.call-done) | copy-start | bytes 38535172
  565.6 19.0 %slice-start = ((s8[12845056]{0:T(1024)(128)(4,1)}), s8[4194304]{0:T(1024)(128)(4,1)S(1)}, s32[]{:S(2)}) async-start(s8[12845056]{0:T(1024)(128)(4,1)} %bitcast.18), calls=%async_computation.9 | async-start | bytes 8388608
  565.6 20.2 %slice-start.1 = ((s8[12845056]{0:T(1024)(128)(4,1)}), s8[4194304]{0:T(1024)(128)(4,1)S(1)}, s32[]{:S(2)}) async-start(s8[12845056]{0:T(1024)(128)(4,1)} %bitcast.18), calls=%async_computation.10 | async-start | bytes 8388608
  578.1 9.0 %slice-start.2 = ((s8[12845056]{0:T(1024)(128)(4,1)}), s8[4194304]{0:T(1024)(128)(4,1)S(1)}, s32[]{:S(2)}) async-start(s8[12845056]{0:T(1024)(128)(4,1)} %bitcast.18), calls=%async_computation.11 | async-start | bytes 8388608
  578.1 9.0 %slice-start.3 = ((s8[12845056]{0:T(1024)(128)(4,1)}), s8[262144]{0:T(1024)(128)(4,1)S(1)}, s32[]{:S(2)}) async-start(s8[12845056]{0:T(1024)(128)(4,1)} %bitcast.18), calls=%async_computation.12 | async-start | bytes 524288
Sparse Core Ops, SparseCore 0:
  68.7 81.3 reduce-scatter.9
  153.1 76.9 reduce-scatter.11
  232.5 76.9 reduce-scatter.7
  342.3 74.9 all-gather.7
  419.4 72.0 all-gather.3
  493.5 72.0 all-gather.5
where the time goes:
time: 599 us
  waiting for transfers between devices  386 us (64%)
  local copies, waits for them, and re-layouts  154 us (26%)
  blocking collectives  24.7 us (4%)
  between operations  16.9 us (3%)
  other arithmetic  16.2 us (3%)
    all_gather x3, waiting for transfers between devices, step(): whole = [lax.all_gather(one[0], 'dp', axis=1, tiled=True) for one in new]  214 us
    unnamed x23, local copies, waits for them, and re-layouts  154 us
    unnamed x8, waiting for transfers between devices  97.6 us
    reduce_scatter x1, waiting for transfers between devices, step(): lax.psum_scatter(t[0], 'dp', scatter_dimension=1, tiled=True)  74.5 us
    psum x1, blocking collectives, step(): squares = lax.psum(sum((jnp.sum(g * g) for g in gradients)), 'dp')  24.7 us
    convert_element_type x3, other arithmetic, adamw(): return ((w - 0.02 * step).astype(jnp.bfloat16), m, v)  13.1 us
  transfers between devices with their start and end apart: 6, of which 6 were waited for; matrix products, arithmetic and copies ran while one was open for 13% of the time, Pallas kernels for 0%

commit v1 on v0

v1 whole, which is shorter than its diff:
```python
import functools
import math

import jax
import jax.numpy as jnp
from jax import lax
from jax.experimental import pallas as pl
from jax.experimental.pallas import tpu as pltpu
from jax.sharding import PartitionSpec as P

MESH = pl.DeviceIdType.MESH
CORES = 2
ROWS, LANES = 8, 128
SLAB = 28
F32 = jnp.float32


def adamw(w, m, v, g):
    m = 0.9 * m + 0.1 * g
    v = 0.95 * v + 0.05 * g * g
    step = m * lax.rsqrt(v + 1e-8) + 0.1 * w
    return (w - 0.02 * step).astype(jnp.bfloat16), m, v


def slabs(ref, body, start=None):
    tiles, columns = ref.shape[0], ref.shape[2]
    size = math.gcd(tiles, max(1, SLAB * LANES // columns))
    return lax.fori_loop(0, tiles // size, lambda i, so_far: body(pl.ds(i * size, size), so_far), start)


def kernel(*refs):
    terms, weights, m_in, v_in, whole, m, v, own, g, w, (squares, pair_send, pair_recv, ring_send, ring_recv, own_sem, load_sem, norm_send, norm_recv) = (
        *(refs[i : i + 3] for i in range(0, 30, 3)),
        refs[30:],
    )
    layers, group = whole[0].shape[:2]
    chips = group // CORES
    count = group * sum(math.prod(one.shape) for one in g)
    me = lax.axis_index("dp")
    core, z = lax.rem(me, CORES), lax.div(me, CORES)
    partner = z * CORES + (1 - core)
    chunks = [(i, l) for i in range(3) for l in range(layers)]

    def away(l, steps):
        return lax.rem(z + (steps if l % 2 == 0 else chips - steps), chips)

    def come(l, steps):
        return lax.rem(z + (chips - steps if l % 2 == 0 else steps), chips)

    def remote(src, dst, send, recv, device):
        return pltpu.make_async_remote_copy(src_ref=src, dst_ref=dst, send_sem=send, recv_sem=recv, device_id={"dp": device}, device_id_type=MESH)

    def pair(i, l, s):
        return remote(terms[i].at[l, come(l, s + 1) * CORES + (1 - core)], whole[i].at[l, s], pair_send.at[i, l, s], pair_recv.at[i, l, s], partner)

    def mine(i, l, s):
        return pltpu.make_async_copy(terms[i].at[l, come(l, s + 1) * CORES + core], own[i].at[lax.rem(s, 2), l], own_sem.at[i, l, lax.rem(s, 2)])

    def total(l, s):
        return chips + s - 1

    def send_total(i, l, s):
        src = s if isinstance(s, int) and s == 0 else total(l, s)
        return remote(whole[i].at[l, src], whole[i].at[l, total(l, s + 1)], ring_send.at[i, l, s], ring_recv.at[i, l, s], away(l, 1) * CORES + core)

    def add(i, l, s, first, last):
        if not first:
            send_total(i, l, s - 1).wait_recv()
        mine(i, l, s).wait()
        pair(i, l, s).wait_recv()

        def body(at, so_far):
            value = own[i][lax.rem(s, 2), l, at].astype(F32) + whole[i][l, s, at].astype(F32)
            if not first:
                value += whole[i][l, total(l, s), at].astype(F32)
            value = value.astype(jnp.bfloat16)
            if not last:
                whole[i][l, s if first else total(l, s), at] = value
                return so_far
            g[i][l, at] = value
            value = value.astype(F32)
            value = jnp.sum(value * value, axis=0)
            for column in range(0, value.shape[1], LANES):
                so_far += value[:, column : column + LANES]
            return so_far

        return slabs(g[i].at[l], body, jnp.zeros((ROWS, LANES), F32) if last else None)

    for i, l in chunks:
        mine(i, l, 0).start()
    barrier = pltpu.get_barrier_semaphore()
    for other in range(1, group):
        pl.semaphore_signal(barrier, inc=1, device_id={"dp": lax.rem(me + other, group)}, device_id_type=MESH)
    pl.semaphore_wait(barrier, group - 1)
    for s in range(2):
        for i, l in chunks:
            pair(i, l, s).start()

    def loads():
        for i in range(3):
            yield pltpu.make_async_copy(m_in[i], m[i], load_sem.at[i, 0])
            yield pltpu.make_async_copy(v_in[i], v[i], load_sem.at[i, 1])
            for l in range(layers):
                yield pltpu.make_async_copy(weights[i].at[l, me], w[i].at[l], load_sem.at[i, 2 + l])

    def step(s, first):
        for i, l in chunks:
            mine(i, l, s + 1).start()
        for i, l in chunks:
            add(i, l, s, first, False)
            send_total(i, l, s).start()

    step(0, True)
    for load in loads():
        load.start()

    @pl.loop(1, chips - 1)
    def _(s):
        for i, l in chunks:
            pair(i, l, s + 1).start()
        step(s, False)

    square = jnp.zeros((ROWS, LANES), F32)
    for i, l in chunks:
        square += add(i, l, chips - 1, False, True)
    squares[me] = square

    @pl.loop(0, chips)
    def _(s):
        for i, l in chunks:
            pair(i, l, s).wait_send()

    send_wait = lambda i, l, s: remote(whole[i].at[l, s], whole[i].at[l, s], ring_send.at[i, l, s], ring_recv.at[i, l, s], away(l, 1) * CORES + core).wait_send()

    @pl.loop(0, chips - 1)
    def _(s):
        for i, l in chunks:
            send_wait(i, l, s)

    def norm(to, source):
        return remote(squares.at[source], squares.at[source], norm_send.at[to], norm_recv.at[source], to)

    for other in range(1, group):
        norm(lax.rem(me + other, group), me).start()
    for load in loads():
        load.wait()
    for other in range(1, group):
        norm(lax.rem(me + other, group), lax.rem(me + other, group)).wait_recv()
    square = jnp.sum(jnp.sum(squares[...], axis=0), axis=(0, 1), keepdims=True)
    factor = jnp.minimum(1.0, 0.5 * lax.rsqrt(square / count + 1e-30))[None]

    def ring(i, l, s):
        slot = whole[i].at[l, come(l, s) * CORES + core]
        return remote(slot, slot, ring_send.at[i, l, s], ring_recv.at[i, l, s], away(l, 1) * CORES + core)

    def share(i, l, s):
        slot = whole[i].at[l, come(l, s) * CORES + core]
        return remote(slot, slot, pair_send.at[i, l, s], pair_recv.at[i, l, s], partner)

    for i, l in chunks:

        def body(at, so_far):
            new = adamw(w[i][l, at].astype(F32), m[i][l, at], v[i][l, at], g[i][l, at].astype(F32) * factor)
            whole[i][l, me, at], m[i][l, at], v[i][l, at] = new
            return so_far

        slabs(g[i].at[l], body)
        ring(i, l, 0).start()
        share(i, l, 0).start()

    @pl.loop(1, chips - 1)
    def _(s):
        for i, l in chunks:
            ring(i, l, s - 1).wait_recv()
            ring(i, l, s).start()
            share(i, l, s).start()

    for i, l in chunks:
        ring(i, l, chips - 2).wait_recv()
        share(i, l, chips - 1).start()

    for other in range(1, group):
        norm(lax.rem(me + other, group), me).wait_send()

    @pl.loop(0, chips - 1)
    def _(s):
        for i, l in chunks:
            ring(i, l, s).wait_send()

    @pl.loop(0, chips)
    def _(s):
        for i, l in chunks:
            share(i, l, s).wait_send()
            share(i, l, s).wait_recv()


def write(*refs):
    half = (len(refs) - 1) // 2
    copies = [pltpu.make_async_copy(src, dst, refs[-1].at[i]) for i, (src, dst) in enumerate(zip(refs[:half], refs[half : 2 * half], strict=True))]
    for copy in copies:
        copy.start()
    for copy in copies:
        copy.wait()


def solution(mesh):
    group = mesh.shape["dp"]
    chips = group // CORES

    def step(*arrays):
        terms, weights, m, v = (arrays[i : i + 3] for i in (0, 3, 6, 9))
        layers = terms[0].shape[1]
        chunk = [(one.shape[1] // ROWS, ROWS, one.shape[2]) for one in m]
        blocks = [(layers, group, *one) for one in chunk]
        local = [(layers, *one) for one in chunk]
        terms = [one.reshape(shape) for one, shape in zip(terms, blocks, strict=True)]
        old = [one.reshape(shape) for one, shape in zip(weights, blocks, strict=True)]
        moments = [one.reshape(shape) for one, shape in zip(m + v, local * 2, strict=True)]
        kept = [pltpu.VMEM(shape, jnp.bfloat16) for shape in blocks] + [pltpu.VMEM(shape, F32) for shape in local * 2]
        elements = sum(math.prod(shape) for shape in blocks)
        new = pl.pallas_call(
            kernel,
            out_shape=kept,
            in_specs=[pl.BlockSpec(memory_space=pltpu.HBM)] * 12,
            out_specs=[pl.BlockSpec(memory_space=pltpu.VMEM)] * 9,
            scratch_shapes=[
                *(pltpu.VMEM((2, *shape), jnp.bfloat16) for shape in local),
                *(pltpu.VMEM(shape, jnp.bfloat16) for shape in local * 2),
                pltpu.VMEM((group, ROWS, LANES), F32),
                *[pltpu.SemaphoreType.DMA((3, layers, chips))] * 4,
                pltpu.SemaphoreType.DMA((3, layers, 2)),
                pltpu.SemaphoreType.DMA((3, 2 + layers)),
                *[pltpu.SemaphoreType.DMA((group,))] * 2,
            ],
            compiler_params=pltpu.CompilerParams(collective_id=0, has_side_effects=True, vmem_limit_bytes=12 * 2**20),
            cost_estimate=pl.CostEstimate(flops=20 * elements, bytes_accessed=4 * elements, transcendentals=elements // group),
        )(*terms, *old, *moments)
        out = pl.pallas_call(
            write,
            out_shape=[jax.ShapeDtypeStruct(one.shape, one.dtype) for one in new],
            in_specs=[pl.BlockSpec(memory_space=pl.ANY)] * 9,
            out_specs=[pl.BlockSpec(memory_space=pl.ANY)] * 9,
            scratch_shapes=[pltpu.SemaphoreType.DMA((9,))],
            compiler_params=pltpu.CompilerParams(vmem_limit_bytes=12 * 2**20, has_side_effects=True),
        )(*new)
        return tuple(one.reshape(like.shape) for one, like in zip(out, weights + m + v, strict=True))

    all_of, cut = P(None, None, None), P(None, "dp", None)
    return jax.shard_map(
        step,
        mesh=mesh,
        in_specs=(P(("rep", "dp"), None, None, None),) * 3 + (all_of,) * 3 + (cut,) * 6,
        out_specs=(P("rep", None, None),) * 3 + (P("rep", "dp", None),) * 6,
        check_vma=False,
    )
```

time: 599 us -> 784 us (1.31)
  Pallas kernels: 0 us -> 779 us
  waiting for transfers between devices: 386 us -> 0 us
  local copies, waits for them, and re-layouts: 154 us -> 4.6 us
  blocking collectives: 24.7 us -> 0 us
  between operations: 16.9 us -> 0.66 us
  other arithmetic: 16.2 us -> 0 us
    pallas_call x0 -> x2, Pallas kernels: none -> 779 us  [the longest x1 390 us: step(): pl.pallas_call(write, out_shape=[jax.ShapeDtypeStruct(one.shape, one.dtyp...]
    all_gather x3 -> x0, waiting for transfers between devices: 214 us -> none  [step(): whole = [lax.all_gather(one[0], 'dp', axis=1, tiled=True) for one in new]]
    unnamed x23 -> x2, local copies, waits for them, and re-layouts: 154 us -> 4.6 us
    unnamed x8 -> x0, waiting for transfers between devices: 97.6 us -> none
    reduce_scatter x1 -> x0, waiting for transfers between devices: 74.5 us -> none  [step(): lax.psum_scatter(t[0], 'dp', scatter_dimension=1, tiled=True)]
    psum x1 -> x0, blocking collectives: 24.7 us -> none  [step(): squares = lax.psum(sum((jnp.sum(g * g) for g in gradients)), 'dp')]
    convert_element_type x3 -> x0, other arithmetic: 13.1 us -> none  [adamw(): return ((w - 0.02 * step).astype(jnp.bfloat16), m, v)]
  transfers between devices with their start and end apart: 6 -> 0, of which waited for: 6 -> 0; matrix products, arithmetic and copies ran while one was open for 13% -> 0% of each run, Pallas kernels for 0% -> 0%
where the time goes in v1:
time: 784 us
  Pallas kernels  779 us (99%)
    pallas_call x1, Pallas kernels, step(): pl.pallas_call(write, out_shape=[jax.ShapeDtypeStruct(one.shape, one.dtyp...  390 us
    pallas_call x1, Pallas kernels, step(): pl.pallas_call(kernel, out_shape=kept, in_specs=[pl.BlockSpec(memory_spac...  388 us

profile of v1, /device:TPU:21, one launch (start us, length us, event | category | flops | bytes accessed | tf_op | source)
XLA Modules:
  0.0 784.0 jit_solution(280787053908993947)
XLA Ops:
  0.6 388.4 %shard_map.187 = (bf16[2,16,7,8,3584]{4,3,2,1,0:T(8,128)(2,1)S(1)}, bf16[2,16,7,8,3584]{4,3,2,1,0:T(8,128)(2,1)S(1)}, bf16[2,16,28,8,896]{4,3,2,1,0:T(8,128)(2,1...) custom-call(bf16[2,16,7,8,3584]{4,3,2,1,0:T(8,128)(2,1)} %bitcast.21, ...), custom_call_target="tpu_custom_call" | custom-call | flops 385351680 | bytes 77070336 | tf_op jit(solution)/shard_map/pallas_call | solution.py:221
  389.1 0.0 copy-start
  389.1 4.6 copy-done
  393.7 390.3 %shard_map.188 = (bf16[2,16,7,8,3584]{4,3,2,1,0:T(8,128)(2,1)}, bf16[2,16,7,8,3584]{4,3,2,1,0:T(8,128)(2,1)}, bf16[2,16,28,8,896]{4,3,2,1,0:T(8,128)(2,1)}, f32[...) custom-call(bf16[2,16,7,8,3584]{4,3,2,1,0:T(8,128)(2,1)S(1)} %get-tu, ...), custom_call_target="tpu_custom_call" | custom-call | tf_op jit(solution)/shard_map/pallas_call | solution.py:238
Async XLA Ops:
  389.1 4.6 copy-start

commit v2 on v1

--- a/solution.py
+++ b/solution.py
@@ -29,13 +29,17 @@
 
 
 def kernel(*refs):
-    terms, weights, m_in, v_in, whole, m, v, own, g, w, (squares, pair_send, pair_recv, ring_send, ring_recv, own_sem, load_sem, norm_send, norm_recv) = (
-        *(refs[i : i + 3] for i in range(0, 30, 3)),
-        refs[30:],
-    )
-    layers, group = whole[0].shape[:2]
+    layers = refs[0].shape[0]
+    inputs, flat, rest = refs[:12], refs[12 : 12 + 3 * layers], refs[12 + 3 * layers :]
+    terms, weights, m_in, v_in = (inputs[i : i + 3] for i in range(0, 12, 3))
+    whole = [flat[i : i + layers] for i in range(0, 3 * layers, layers)]
+    m, v, own = (rest[i : i + 3] for i in range(0, 9, 3))
+    squares, pair_send, pair_recv, ring_send, ring_recv, own_sem, load_sem, norm_send, norm_recv = rest[9:]
+    group = terms[0].shape[1]
     chips = group // CORES
-    count = group * sum(math.prod(one.shape) for one in g)
+    count = group * sum(math.prod(one.shape) for one in m)
+    end = (chips - 1) % 2
+    g, w = ([one.at[slot] for one in own] for slot in (end, 1 - end))
     me = lax.axis_index("dp")
     core, z = lax.rem(me, CORES), lax.div(me, CORES)
     partner = z * CORES + (1 - core)
@@ -51,7 +55,7 @@
         return pltpu.make_async_remote_copy(src_ref=src, dst_ref=dst, send_sem=send, recv_sem=recv, device_id={"dp": device}, device_id_type=MESH)
 
     def pair(i, l, s):
-        return remote(terms[i].at[l, come(l, s + 1) * CORES + (1 - core)], whole[i].at[l, s], pair_send.at[i, l, s], pair_recv.at[i, l, s], partner)
+        return remote(terms[i].at[l, come(l, s + 1) * CORES + (1 - core)], whole[i][l].at[s], pair_send.at[i, l, s], pair_recv.at[i, l, s], partner)
 
     def mine(i, l, s):
         return pltpu.make_async_copy(terms[i].at[l, come(l, s + 1) * CORES + core], own[i].at[lax.rem(s, 2), l], own_sem.at[i, l, lax.rem(s, 2)])
@@ -61,7 +65,7 @@
 
     def send_total(i, l, s):
         src = s if isinstance(s, int) and s == 0 else total(l, s)
-        return remote(whole[i].at[l, src], whole[i].at[l, total(l, s + 1)], ring_send.at[i, l, s], ring_recv.at[i, l, s], away(l, 1) * CORES + core)
+        return remote(whole[i][l].at[src], whole[i][l].at[total(l, s + 1)], ring_send.at[i, l, s], ring_recv.at[i, l, s], away(l, 1) * CORES + core)
 
     def add(i, l, s, first, last):
         if not first:
@@ -70,12 +74,12 @@
         pair(i, l, s).wait_recv()
 
         def body(at, so_far):
-            value = own[i][lax.rem(s, 2), l, at].astype(F32) + whole[i][l, s, at].astype(F32)
+            value = own[i][lax.rem(s, 2), l, at].astype(F32) + whole[i][l][s, at].astype(F32)
             if not first:
-                value += whole[i][l, total(l, s), at].astype(F32)
+                value += whole[i][l][total(l, s), at].astype(F32)
             value = value.astype(jnp.bfloat16)
             if not last:
-                whole[i][l, s if first else total(l, s), at] = value
+                whole[i][l][s if first else total(l, s), at] = value
                 return so_far
             g[i][l, at] = value
             value = value.astype(F32)
@@ -84,7 +88,7 @@
                 so_far += value[:, column : column + LANES]
             return so_far
 
-        return slabs(g[i].at[l], body, jnp.zeros((ROWS, LANES), F32) if last else None)
+        return slabs(m[i].at[l], body, jnp.zeros((ROWS, LANES), F32) if last else None)
 
     for i, l in chunks:
         mine(i, l, 0).start()
@@ -96,12 +100,8 @@
         for i, l in chunks:
             pair(i, l, s).start()
 
-    def loads():
-        for i in range(3):
-            yield pltpu.make_async_copy(m_in[i], m[i], load_sem.at[i, 0])
-            yield pltpu.make_async_copy(v_in[i], v[i], load_sem.at[i, 1])
-            for l in range(layers):
-                yield pltpu.make_async_copy(weights[i].at[l, me], w[i].at[l], load_sem.at[i, 2 + l])
+    moments = [pltpu.make_async_copy(src[i], dst[i], load_sem.at[i, k]) for i in range(3) for k, (src, dst) in enumerate(((m_in, m), (v_in, v)))]
+    old = [pltpu.make_async_copy(weights[i].at[l, me], w[i].at[l], load_sem.at[i, 2 + l]) for i, l in chunks]
 
     def step(s, first):
         for i, l in chunks:
@@ -111,7 +111,7 @@
             send_total(i, l, s).start()
 
     step(0, True)
-    for load in loads():
+    for load in moments:
         load.start()
 
     @pl.loop(1, chips - 1)
@@ -120,6 +120,8 @@
             pair(i, l, s + 1).start()
         step(s, False)
 
+    for load in old:
+        load.start()
     square = jnp.zeros((ROWS, LANES), F32)
     for i, l in chunks:
         square += add(i, l, chips - 1, False, True)
@@ -130,7 +132,7 @@
         for i, l in chunks:
             pair(i, l, s).wait_send()
 
-    send_wait = lambda i, l, s: remote(whole[i].at[l, s], whole[i].at[l, s], ring_send.at[i, l, s], ring_recv.at[i, l, s], away(l, 1) * CORES + core).wait_send()
+    send_wait = lambda i, l, s: remote(whole[i][l].at[s], whole[i][l].at[s], ring_send.at[i, l, s], ring_recv.at[i, l, s], away(l, 1) * CORES + core).wait_send()
 
     @pl.loop(0, chips - 1)
     def _(s):
@@ -142,7 +144,7 @@
 
     for other in range(1, group):
         norm(lax.rem(me + other, group), me).start()
-    for load in loads():
+    for load in (*moments, *old):
         load.wait()
     for other in range(1, group):
         norm(lax.rem(me + other, group), lax.rem(me + other, group)).wait_recv()
@@ -150,21 +152,21 @@
     factor = jnp.minimum(1.0, 0.5 * lax.rsqrt(square / count + 1e-30))[None]
 
     def ring(i, l, s):
-        slot = whole[i].at[l, come(l, s) * CORES + core]
+        slot = whole[i][l].at[come(l, s) * CORES + core]
         return remote(slot, slot, ring_send.at[i, l, s], ring_recv.at[i, l, s], away(l, 1) * CORES + core)
 
     def share(i, l, s):
-        slot = whole[i].at[l, come(l, s) * CORES + core]
+        slot = whole[i][l].at[come(l, s) * CORES + core]
         return remote(slot, slot, pair_send.at[i, l, s], pair_recv.at[i, l, s], partner)
 
     for i, l in chunks:
 
         def body(at, so_far):
             new = adamw(w[i][l, at].astype(F32), m[i][l, at], v[i][l, at], g[i][l, at].astype(F32) * factor)
-            whole[i][l, me, at], m[i][l, at], v[i][l, at] = new
+            whole[i][l][me, at], m[i][l, at], v[i][l, at] = new
             return so_far
 
-        slabs(g[i].at[l], body)
+        slabs(m[i].at[l], body)
         ring(i, l, 0).start()
         share(i, l, 0).start()
 
@@ -194,9 +196,12 @@
             share(i, l, s).wait_recv()
 
 
-def write(*refs):
-    half = (len(refs) - 1) // 2
-    copies = [pltpu.make_async_copy(src, dst, refs[-1].at[i]) for i, (src, dst) in enumerate(zip(refs[:half], refs[half : 2 * half], strict=True))]
+def write(layers, *refs):
+    *refs, sem = refs
+    src, dst = refs[:-9], refs[-9:]
+    pieces = [(src[i * layers + l], dst[i].at[l]) for i in range(3) for l in range(layers)]
+    pieces += zip(src[3 * layers :], dst[3:], strict=True)
+    copies = [pltpu.make_async_copy(*piece, sem.at[i]) for i, piece in enumerate(pieces)]
     for copy in copies:
         copy.start()
     for copy in copies:
@@ -216,32 +221,31 @@
         terms = [one.reshape(shape) for one, shape in zip(terms, blocks, strict=True)]
         old = [one.reshape(shape) for one, shape in zip(weights, blocks, strict=True)]
         moments = [one.reshape(shape) for one, shape in zip(m + v, local * 2, strict=True)]
-        kept = [pltpu.VMEM(shape, jnp.bfloat16) for shape in blocks] + [pltpu.VMEM(shape, F32) for shape in local * 2]
+        kept = [pltpu.VMEM(shape[1:], jnp.bfloat16) for shape in blocks for _ in range(layers)] + [pltpu.VMEM(shape, F32) for shape in local * 2]
         elements = sum(math.prod(shape) for shape in blocks)
         new = pl.pallas_call(
             kernel,
             out_shape=kept,
             in_specs=[pl.BlockSpec(memory_space=pltpu.HBM)] * 12,
-            out_specs=[pl.BlockSpec(memory_space=pltpu.VMEM)] * 9,
+            out_specs=[pl.BlockSpec(memory_space=pltpu.VMEM)] * len(kept),
             scratch_shapes=[
                 *(pltpu.VMEM((2, *shape), jnp.bfloat16) for shape in local),
-                *(pltpu.VMEM(shape, jnp.bfloat16) for shape in local * 2),
                 pltpu.VMEM((group, ROWS, LANES), F32),
                 *[pltpu.SemaphoreType.DMA((3, layers, chips))] * 4,
                 pltpu.SemaphoreType.DMA((3, layers, 2)),
                 pltpu.SemaphoreType.DMA((3, 2 + layers)),
                 *[pltpu.SemaphoreType.DMA((group,))] * 2,
             ],
-            compiler_params=pltpu.CompilerParams(collective_id=0, has_side_effects=True, vmem_limit_bytes=12 * 2**20),
+            compiler_params=pltpu.CompilerParams(collective_id=0, has_side_effects=True, vmem_limit_bytes=8 * 2**20),
             cost_estimate=pl.CostEstimate(flops=20 * elements, bytes_accessed=4 * elements, transcendentals=elements // group),
         )(*terms, *old, *moments)
         out = pl.pallas_call(
-            write,
-            out_shape=[jax.ShapeDtypeStruct(one.shape, one.dtype) for one in new],
-            in_specs=[pl.BlockSpec(memory_space=pl.ANY)] * 9,
+            functools.partial(write, layers),
+            out_shape=[jax.ShapeDtypeStruct(shape, jnp.bfloat16) for shape in blocks] + [jax.ShapeDtypeStruct(shape, F32) for shape in local * 2],
+            in_specs=[pl.BlockSpec(memory_space=pl.ANY)] * len(kept),
             out_specs=[pl.BlockSpec(memory_space=pl.ANY)] * 9,
-            scratch_shapes=[pltpu.SemaphoreType.DMA((9,))],
-            compiler_params=pltpu.CompilerParams(vmem_limit_bytes=12 * 2**20, has_side_effects=True),
+            scratch_shapes=[pltpu.SemaphoreType.DMA((len(kept),))],
+            compiler_params=pltpu.CompilerParams(vmem_limit_bytes=8 * 2**20),
         )(*new)
         return tuple(one.reshape(like.shape) for one, like in zip(out, weights + m + v, strict=True))
 

time: 784 us -> 405 us (0.52)
  Pallas kernels: 779 us -> 404 us
    pallas_call x1, Pallas kernels: 390 us -> 15.5 us  [step(): pl.pallas_call(functools.partial(write, layers), out_shape=[jax.ShapeDtyp...]
where the time goes in v2:
time: 405 us
  Pallas kernels  404 us (100%)
    pallas_call x1, Pallas kernels, step(): pl.pallas_call(kernel, out_shape=kept, in_specs=[pl.BlockSpec(memory_spac...  388 us
    pallas_call x1, Pallas kernels, step(): pl.pallas_call(functools.partial(write, layers), out_shape=[jax.ShapeDtyp...  15.5 us

profile of v2, /device:TPU:21, one launch (start us, length us, event | category | flops | bytes accessed | tf_op | source)
XLA Modules:
  0.0 404.5 jit_solution(14717513562068733854)
XLA Ops:
  0.6 388.4 %shard_map.187 = (bf16[16,7,8,3584]{3,2,1,0:T(8,128)(2,1)S(1)}, bf16[16,7,8,3584]{3,2,1,0:T(8,128)(2,1)S(1)}, bf16[16,7,8,3584]{3,2,1,0:T(8,128)(2,1)S(1)}, bf16...) custom-call(bf16[2,16,7,8,3584]{4,3,2,1,0:T(8,128)(2,1)} %bitcast.21, ...), custom_call_target="tpu_custom_call" | custom-call | flops 385351680 | bytes 77070336 | tf_op jit(solution)/shard_map/pallas_call | solution.py:226
  389.1 15.5 %shard_map.188 = (bf16[2,16,7,8,3584]{4,3,2,1,0:T(8,128)(2,1)}, bf16[2,16,7,8,3584]{4,3,2,1,0:T(8,128)(2,1)}, bf16[2,16,28,8,896]{4,3,2,1,0:T(8,128)(2,1)}, f32[...) custom-call(bf16[16,7,8,3584]{3,2,1,0:T(8,128)(2,1)S(1)} %get-tuple-, ...), custom_call_target="tpu_custom_call" | custom-call | tf_op jit(solution)/shard_map/pallas_call | solution.py:242

commit v3 on v2

--- a/solution.py
+++ b/solution.py
@@ -34,7 +34,7 @@
     terms, weights, m_in, v_in = (inputs[i : i + 3] for i in range(0, 12, 3))
     whole = [flat[i : i + layers] for i in range(0, 3 * layers, layers)]
     m, v, own = (rest[i : i + 3] for i in range(0, 9, 3))
-    squares, pair_send, pair_recv, ring_send, ring_recv, own_sem, load_sem, norm_send, norm_recv = rest[9:]
+    squares, pair_send, pair_recv, ring_send, ring_recv, own_sem, stage_sem, load_sem, norm_send, norm_recv = rest[9:]
     group = terms[0].shape[1]
     chips = group // CORES
     count = group * sum(math.prod(one.shape) for one in m)
@@ -54,8 +54,12 @@
     def remote(src, dst, send, recv, device):
         return pltpu.make_async_remote_copy(src_ref=src, dst_ref=dst, send_sem=send, recv_sem=recv, device_id={"dp": device}, device_id_type=MESH)
 
+    def stage(i, l):
+        return pltpu.make_async_copy(terms[i].at[l, come(l, 1) * CORES + (1 - core)], whole[i][l].at[group - 1], stage_sem.at[i, l])
+
     def pair(i, l, s):
-        return remote(terms[i].at[l, come(l, s + 1) * CORES + (1 - core)], whole[i][l].at[s], pair_send.at[i, l, s], pair_recv.at[i, l, s], partner)
+        first = isinstance(s, int) and s == 0
+        return remote(whole[i][l].at[group - 1] if first else terms[i].at[l, come(l, s + 1) * CORES + (1 - core)], whole[i][l].at[s], pair_send.at[i, l, s], pair_recv.at[i, l, s], partner)
 
     def mine(i, l, s):
         return pltpu.make_async_copy(terms[i].at[l, come(l, s + 1) * CORES + core], own[i].at[lax.rem(s, 2), l], own_sem.at[i, l, lax.rem(s, 2)])
@@ -91,14 +95,17 @@
         return slabs(m[i].at[l], body, jnp.zeros((ROWS, LANES), F32) if last else None)
 
     for i, l in chunks:
+        stage(i, l).start()
         mine(i, l, 0).start()
     barrier = pltpu.get_barrier_semaphore()
-    for other in range(1, group):
-        pl.semaphore_signal(barrier, inc=1, device_id={"dp": lax.rem(me + other, group)}, device_id_type=MESH)
-    pl.semaphore_wait(barrier, group - 1)
-    for s in range(2):
-        for i, l in chunks:
-            pair(i, l, s).start()
+    for other in (partner, away(0, 1) * CORES + core, come(0, 1) * CORES + core):
+        pl.semaphore_signal(barrier, inc=1, device_id={"dp": other}, device_id_type=MESH)
+    pl.semaphore_wait(barrier, 3)
+    for i, l in chunks:
+        stage(i, l).wait()
+        pair(i, l, 0).start()
+    for i, l in chunks:
+        pair(i, l, 1).start()
 
     moments = [pltpu.make_async_copy(src[i], dst[i], load_sem.at[i, k]) for i in range(3) for k, (src, dst) in enumerate(((m_in, m), (v_in, v)))]
     old = [pltpu.make_async_copy(weights[i].at[l, me], w[i].at[l], load_sem.at[i, 2 + l]) for i, l in chunks]
@@ -122,22 +129,26 @@
 
     for load in old:
         load.start()
+
+    def sent(i, l, s):
+        slot = whole[i][l].at[s]
+        return remote(slot, slot, ring_send.at[i, l, s], ring_recv.at[i, l, s], away(l, 1) * CORES + core)
+
+    @pl.loop(0, chips - 2)
+    def _(s):
+        for i, l in chunks:
+            pair(i, l, s).wait_send()
+            sent(i, l, s).wait_send()
+
+    for i, l in chunks:
+        pair(i, l, chips - 2).wait_send()
     square = jnp.zeros((ROWS, LANES), F32)
     for i, l in chunks:
         square += add(i, l, chips - 1, False, True)
-    squares[me] = square
-
-    @pl.loop(0, chips)
-    def _(s):
-        for i, l in chunks:
-            pair(i, l, s).wait_send()
-
-    send_wait = lambda i, l, s: remote(whole[i][l].at[s], whole[i][l].at[s], ring_send.at[i, l, s], ring_recv.at[i, l, s], away(l, 1) * CORES + core).wait_send()
-
-    @pl.loop(0, chips - 1)
-    def _(s):
-        for i, l in chunks:
-            send_wait(i, l, s)
+    squares[me] = jnp.sum(square, axis=0, keepdims=True)
+    for i, l in chunks:
+        pair(i, l, chips - 1).wait_send()
+        sent(i, l, chips - 2).wait_send()
 
     def norm(to, source):
         return remote(squares.at[source], squares.at[source], norm_send.at[to], norm_recv.at[source], to)
@@ -148,7 +159,7 @@
         load.wait()
     for other in range(1, group):
         norm(lax.rem(me + other, group), lax.rem(me + other, group)).wait_recv()
-    square = jnp.sum(jnp.sum(squares[...], axis=0), axis=(0, 1), keepdims=True)
+    square = jnp.sum(jnp.sum(squares[...], axis=0), axis=1, keepdims=True)
     factor = jnp.minimum(1.0, 0.5 * lax.rsqrt(square / count + 1e-30))[None]
 
     def ring(i, l, s):
@@ -177,21 +188,23 @@
             ring(i, l, s).start()
             share(i, l, s).start()
 
+    for other in range(1, group):
+        norm(lax.rem(me + other, group), me).wait_send()
+
+    @pl.loop(0, chips - 2)
+    def _(s):
+        for i, l in chunks:
+            ring(i, l, s).wait_send()
+            share(i, l, s).wait_send()
+            share(i, l, s).wait_recv()
+
     for i, l in chunks:
         ring(i, l, chips - 2).wait_recv()
         share(i, l, chips - 1).start()
-
-    for other in range(1, group):
-        norm(lax.rem(me + other, group), me).wait_send()
-
-    @pl.loop(0, chips - 1)
-    def _(s):
-        for i, l in chunks:
-            ring(i, l, s).wait_send()
-
-    @pl.loop(0, chips)
-    def _(s):
-        for i, l in chunks:
+    for s in (chips - 2, chips - 1):
+        for i, l in chunks:
+            if s < chips - 1:
+                ring(i, l, s).wait_send()
             share(i, l, s).wait_send()
             share(i, l, s).wait_recv()
 
@@ -230,9 +243,10 @@
             out_specs=[pl.BlockSpec(memory_space=pltpu.VMEM)] * len(kept),
             scratch_shapes=[
                 *(pltpu.VMEM((2, *shape), jnp.bfloat16) for shape in local),
-                pltpu.VMEM((group, ROWS, LANES), F32),
+                pltpu.VMEM((group, 1, LANES), F32),
                 *[pltpu.SemaphoreType.DMA((3, layers, chips))] * 4,
                 pltpu.SemaphoreType.DMA((3, layers, 2)),
+                pltpu.SemaphoreType.DMA((3, layers)),
                 pltpu.SemaphoreType.DMA((3, 2 + layers)),
                 *[pltpu.SemaphoreType.DMA((group,))] * 2,
             ],

time: 405 us -> 402 us (level)
  no operation moved by 1% of the time
where the time goes in v3:
time: 402 us
  Pallas kernels  401 us (100%)
    pallas_call x1, Pallas kernels, step(): pl.pallas_call(kernel, out_shape=kept, in_specs=[pl.BlockSpec(memory_spac...  386 us
    pallas_call x1, Pallas kernels, step(): pl.pallas_call(functools.partial(write, layers), out_shape=[jax.ShapeDtyp...  15.5 us

profile of v3, /device:TPU:21, one launch (start us, length us, event | category | flops | bytes accessed | tf_op | source)
XLA Modules:
  0.0 401.8 jit_solution(2603709186262771644)
XLA Ops:
  0.6 385.7 %shard_map.187 = (bf16[16,7,8,3584]{3,2,1,0:T(8,128)(2,1)S(1)}, bf16[16,7,8,3584]{3,2,1,0:T(8,128)(2,1)S(1)}, bf16[16,7,8,3584]{3,2,1,0:T(8,128)(2,1)S(1)}, bf16...) custom-call(bf16[2,16,7,8,3584]{4,3,2,1,0:T(8,128)(2,1)} %bitcast.21, ...), custom_call_target="tpu_custom_call" | custom-call | flops 385351680 | bytes 77070336 | tf_op jit(solution)/shard_map/pallas_call | solution.py:239
  386.3 15.5 %shard_map.188 = (bf16[2,16,7,8,3584]{4,3,2,1,0:T(8,128)(2,1)}, bf16[2,16,7,8,3584]{4,3,2,1,0:T(8,128)(2,1)}, bf16[2,16,28,8,896]{4,3,2,1,0:T(8,128)(2,1)}, f32[...) custom-call(bf16[16,7,8,3584]{3,2,1,0:T(8,128)(2,1)S(1)} %get-tuple-, ...), custom_call_target="tpu_custom_call" | custom-call | tf_op jit(solution)/shard_map/pallas_call | solution.py:256

commit v4 on v3

--- a/solution.py
+++ b/solution.py
@@ -94,30 +94,26 @@
 
         return slabs(m[i].at[l], body, jnp.zeros((ROWS, LANES), F32) if last else None)
 
-    for i, l in chunks:
-        stage(i, l).start()
-        mine(i, l, 0).start()
     barrier = pltpu.get_barrier_semaphore()
     for other in (partner, away(0, 1) * CORES + core, come(0, 1) * CORES + core):
         pl.semaphore_signal(barrier, inc=1, device_id={"dp": other}, device_id_type=MESH)
+    for i, l in chunks:
+        stage(i, l).start()
+        mine(i, l, 0).start()
     pl.semaphore_wait(barrier, 3)
     for i, l in chunks:
         stage(i, l).wait()
         pair(i, l, 0).start()
-    for i, l in chunks:
-        pair(i, l, 1).start()
 
     moments = [pltpu.make_async_copy(src[i], dst[i], load_sem.at[i, k]) for i in range(3) for k, (src, dst) in enumerate(((m_in, m), (v_in, v)))]
     old = [pltpu.make_async_copy(weights[i].at[l, me], w[i].at[l], load_sem.at[i, 2 + l]) for i, l in chunks]
 
-    def step(s, first):
-        for i, l in chunks:
-            mine(i, l, s + 1).start()
-        for i, l in chunks:
-            add(i, l, s, first, False)
-            send_total(i, l, s).start()
-
-    step(0, True)
+    for i, l in chunks:
+        add(i, l, 0, True, False)
+        send_total(i, l, 0).start()
+    for i, l in chunks:
+        pair(i, l, 1).start()
+        mine(i, l, 1).start()
     for load in moments:
         load.start()
 
@@ -125,7 +121,10 @@
     def _(s):
         for i, l in chunks:
             pair(i, l, s + 1).start()
-        step(s, False)
+            mine(i, l, s + 1).start()
+        for i, l in chunks:
+            add(i, l, s, False, False)
+            send_total(i, l, s).start()
 
     for load in old:
         load.start()
@@ -147,14 +146,15 @@
         square += add(i, l, chips - 1, False, True)
     squares[me] = jnp.sum(square, axis=0, keepdims=True)
     for i, l in chunks:
-        pair(i, l, chips - 1).wait_send()
         sent(i, l, chips - 2).wait_send()
 
     def norm(to, source):
         return remote(squares.at[source], squares.at[source], norm_send.at[to], norm_recv.at[source], to)
 
-    for other in range(1, group):
+    for other in sorted(range(1, group), key=lambda other: abs(group // 2 - other)):
         norm(lax.rem(me + other, group), me).start()
+    for i, l in chunks:
+        pair(i, l, chips - 1).wait_send()
     for load in (*moments, *old):
         load.wait()
     for other in range(1, group):

time: 402 us -> 402 us (level)
  no operation moved by 1% of the time
where the time goes in v4:
time: 402 us
  Pallas kernels  401 us (100%)
    pallas_call x1, Pallas kernels, step(): pl.pallas_call(kernel, out_shape=kept, in_specs=[pl.BlockSpec(memory_spac...  386 us
    pallas_call x1, Pallas kernels, step(): pl.pallas_call(functools.partial(write, layers), out_shape=[jax.ShapeDtyp...  15.5 us

profile of v4, /device:TPU:21, one launch (start us, length us, event | category | flops | bytes accessed | tf_op | source)
XLA Modules:
  0.0 401.7 jit_solution(2234487519096432684)
XLA Ops:
  0.6 385.6 %shard_map.187 = (bf16[16,7,8,3584]{3,2,1,0:T(8,128)(2,1)S(1)}, bf16[16,7,8,3584]{3,2,1,0:T(8,128)(2,1)S(1)}, bf16[16,7,8,3584]{3,2,1,0:T(8,128)(2,1)S(1)}, bf16...) custom-call(bf16[2,16,7,8,3584]{4,3,2,1,0:T(8,128)(2,1)} %bitcast.21, ...), custom_call_target="tpu_custom_call" | custom-call | flops 385351680 | bytes 77070336 | tf_op jit(solution)/shard_map/pallas_call | solution.py:239
  386.3 15.5 %shard_map.188 = (bf16[2,16,7,8,3584]{4,3,2,1,0:T(8,128)(2,1)}, bf16[2,16,7,8,3584]{4,3,2,1,0:T(8,128)(2,1)}, bf16[2,16,28,8,896]{4,3,2,1,0:T(8,128)(2,1)}, f32[...) custom-call(bf16[16,7,8,3584]{3,2,1,0:T(8,128)(2,1)S(1)} %get-tuple-, ...), custom_call_target="tpu_custom_call" | custom-call | tf_op jit(solution)/shard_map/pallas_call | solution.py:256

commit v5 on v4

--- a/solution.py
+++ b/solution.py
@@ -212,8 +212,8 @@
 def write(layers, *refs):
     *refs, sem = refs
     src, dst = refs[:-9], refs[-9:]
-    pieces = [(src[i * layers + l], dst[i].at[l]) for i in range(3) for l in range(layers)]
-    pieces += zip(src[3 * layers :], dst[3:], strict=True)
+    pieces = list(zip(src[3 * layers :], dst[3:], strict=True))
+    pieces += [(src[i * layers + l], dst[i].at[l]) for i in range(3) for l in range(layers)]
     copies = [pltpu.make_async_copy(*piece, sem.at[i]) for i, piece in enumerate(pieces)]
     for copy in copies:
         copy.start()

time: 402 us -> 402 us (level)
  no operation moved by 1% of the time
where the time goes in v5:
time: 402 us
  Pallas kernels  401 us (100%)
    pallas_call x1, Pallas kernels, step(): pl.pallas_call(kernel, out_shape=kept, in_specs=[pl.BlockSpec(memory_spac...  386 us
    pallas_call x1, Pallas kernels, step(): pl.pallas_call(functools.partial(write, layers), out_shape=[jax.ShapeDtyp...  15.6 us

profile of v5, /device:TPU:21, one launch (start us, length us, event | category | flops | bytes accessed | tf_op | source)
XLA Modules:
  0.0 401.8 jit_solution(14691850609903473247)
XLA Ops:
  0.6 385.6 %shard_map.187 = (bf16[16,7,8,3584]{3,2,1,0:T(8,128)(2,1)S(1)}, bf16[16,7,8,3584]{3,2,1,0:T(8,128)(2,1)S(1)}, bf16[16,7,8,3584]{3,2,1,0:T(8,128)(2,1)S(1)}, bf16...) custom-call(bf16[2,16,7,8,3584]{4,3,2,1,0:T(8,128)(2,1)} %bitcast.21, ...), custom_call_target="tpu_custom_call" | custom-call | flops 385351680 | bytes 77070336 | tf_op jit(solution)/shard_map/pallas_call | solution.py:239
  386.3 15.6 %shard_map.188 = (bf16[2,16,7,8,3584]{4,3,2,1,0:T(8,128)(2,1)}, bf16[2,16,7,8,3584]{4,3,2,1,0:T(8,128)(2,1)}, bf16[2,16,28,8,896]{4,3,2,1,0:T(8,128)(2,1)}, f32[...) custom-call(bf16[16,7,8,3584]{3,2,1,0:T(8,128)(2,1)S(1)} %get-tuple-, ...), custom_call_target="tpu_custom_call" | custom-call | tf_op jit(solution)/shard_map/pallas_call | solution.py:256
